TPU v7x, 256 devices: a whole 4x4x8 slice. The times are simulated.
256 devices in a mesh: row: 16 (over y, z_hi), col: 16 (over x, z_lo, core).
Axes of the slice: x: 4, y: 4, z: 8 (z_hi: 4, z_lo: 2; z = z_hi * 2 + z_lo), core: 2. Of those that a mesh axis runs over, the one named last changes fastest.
Arguments:
- left_act: bfloat16 [1536, 128], P(('row', 'col')), may hold values from -540 to 540
- right_act: bfloat16 [1536, 128], P(('row', 'col')), may hold values from -6 to 6
- norm_gain: float32 [128], replicated, may hold values from 0.25 to 1.75
- norm_bias: float32 [128], replicated, may hold values from -3 to 3
- w_in: bfloat16 [128, 512], replicated, may hold values from -0.5 to 0.5
- b_in: float32 [512], replicated, may hold values from -3 to 3
- w_out: bfloat16 [512, 128], replicated, may hold values from -0.25 to 0.25
- w_bins: bfloat16 [128, 64], replicated, may hold values from -0.5 to 0.5
- labels: int32 [1536, 1536], P('row', 'col'), may hold values from 0 to 63, as said below
Outputs:
- grad_left: float32 [1536, 128], P(('row', 'col'))
- grad_right: float32 [1536, 128], P('col')
- grad_w_in: float32 [128, 512], replicated
- grad_w_out: float32 [512, 128], replicated
- grad_w_bins: float32 [128, 64], replicated
Inputs may be any that keep to these rules, and one draw needn't show every extreme that they name: labels is symmetric: labels[i, j] equals labels[j, i].
All inputs are finite; a program needn't handle non-finite values.
Results may differ from a plain program's by a relative error of at most 0.00039.
Values may be sent and summed in bfloat16 or wider, within the bound.
No kernel may reach another device: no remote copies, remote signals or barrier semaphores. Data moves between devices by JAX's collectives and lax.ppermute only.
A program may use at most 64 MiB of HBM per device.

v0:
```python
import jax
import jax.numpy as jnp
from jax import lax
from jax.sharding import PartitionSpec as P


def from_everyone(value, axis):
    count = lax.axis_size(axis)
    return lax.all_to_all(
        jnp.broadcast_to(value[None], (count, *value.shape)), axis, 0, 0, tiled=True
    )


def laid_out(pieces, dim):
    shape = list(pieces.shape[1:])
    shape[dim] *= pieces.shape[0]
    return jnp.moveaxis(pieces, 0, dim).reshape(shape)


def gather_directly(value, axis, dim):
    pieces = from_everyone(value, axis)
    return laid_out(pieces, dim)


def picked(value, axis, root):
    return lax.dynamic_index_in_dim(lax.all_gather(value, axis), root, 0, keepdims=False)


def over_copies(value, axis):
    return from_everyone(value, axis).sum(axis=0)


def inner(first, second):
    return lax.dot_general(
        first, second, (((0,), (0,)), ((), ())), preferred_element_type=jnp.float32
    )


def outer(first, second):
    return lax.dot_general(
        first, second, (((1,), (1,)), ((), ())), preferred_element_type=jnp.float32
    )


def transition(left_rows, right_cols, gain, bias, w_in, b_in, w_out):
    summed = (
        left_rows.astype(jnp.float32)[:, None, :] + right_cols.astype(jnp.float32)[None, :, :]
    ).reshape(-1, left_rows.shape[1])
    center = summed - jnp.mean(summed, axis=-1, keepdims=True)
    inv_scale = lax.rsqrt(jnp.mean(center * center, axis=-1, keepdims=True) + 1e-05)
    normal_form = center * inv_scale
    normed = (normal_form * gain + bias).astype(jnp.bfloat16)
    pre_act = jnp.dot(normed, w_in, preferred_element_type=jnp.float32) + b_in
    hidden = (pre_act * jax.nn.sigmoid(pre_act)).astype(jnp.bfloat16)
    updated = (summed + jnp.dot(hidden, w_out, preferred_element_type=jnp.float32)).astype(
        jnp.bfloat16
    )
    return (normal_form, inv_scale, normed, pre_act, hidden, updated)


def pair_backward(sym, bin_labels, parts, gain, w_in, w_out, w_bins):
    normal_form, inv_scale, normed, pre_act, hidden, updated = parts
    shifted = sym - jnp.max(sym, axis=-1, keepdims=True)
    expo = jnp.exp(shifted)
    probs = expo / jnp.sum(expo, axis=-1, keepdims=True)
    onehot = (bin_labels[..., None] == lax.iota(jnp.int32, sym.shape[-1])).astype(jnp.float32)
    logit_grad = (2.0 * (probs - onehot)).reshape(-1, sym.shape[-1]).astype(jnp.bfloat16)
    grad_bins = inner(updated, logit_grad)
    upd_grad = outer(logit_grad, w_bins)
    upd_half = upd_grad.astype(jnp.bfloat16)
    grad_out = inner(hidden, upd_half)
    hid_grad = outer(upd_half, w_out)
    sigma = jax.nn.sigmoid(pre_act)
    pre_grad = (hid_grad * sigma * (1.0 + pre_act * (1.0 - sigma))).astype(jnp.bfloat16)
    grad_in = inner(normed, pre_grad)
    norm_grad = outer(pre_grad, w_in) * gain
    pair_grad = (
        inv_scale
        * (
            norm_grad
            - jnp.mean(norm_grad, axis=-1, keepdims=True)
            - normal_form * jnp.mean(norm_grad * normal_form, axis=-1, keepdims=True)
        )
        + upd_grad
    )
    return (grad_in, grad_out, grad_bins, pair_grad)


def on_device(left_act, right_act, norm_gain, norm_bias, w_in, b_in, w_out, w_bins, labels):
    tile_rows, tile_cols = labels.shape
    width = left_act.shape[1]
    stacked = jnp.stack([left_act, right_act])
    row_block = gather_directly(stacked, "col", 1)
    fanout = lax.axis_size("row") // lax.axis_size("col")
    pieces = picked(row_block, "row", lax.axis_index("col") * fanout + 0)
    stride_rows = 8
    groups = tile_rows // stride_rows

    def advance(running, record):
        left_rows, right_rows, bin_labels = record
        own_parts = transition(left_rows, pieces[1], norm_gain, norm_bias, w_in, b_in, w_out)
        own_logits = jnp.dot(own_parts[5], w_bins, preferred_element_type=jnp.float32).reshape(
            stride_rows, tile_cols, -1
        )
        far_parts = transition(pieces[0], right_rows, norm_gain, norm_bias, w_in, b_in, w_out)
        far_logits = jnp.dot(far_parts[5], w_bins, preferred_element_type=jnp.float32).reshape(
            tile_cols, stride_rows, -1
        )
        sym = own_logits + jnp.transpose(far_logits, (1, 0, 2))
        grads = pair_backward(sym, bin_labels, own_parts, norm_gain, w_in, w_out, w_bins)
        pair_grad = grads[3].reshape(stride_rows, tile_cols, width)
        running = (
            running[0] + grads[0],
            running[1] + grads[1],
            running[2] + grads[2],
            running[3] + jnp.sum(pair_grad, axis=0),
        )
        return (running, jnp.sum(pair_grad, axis=1))

    start = (
        jnp.zeros((width, w_in.shape[1]), jnp.float32),
        jnp.zeros((w_in.shape[1], width), jnp.float32),
        jnp.zeros((width, w_bins.shape[1]), jnp.float32),
        jnp.zeros((tile_cols, width), jnp.float32),
    )
    records = (
        row_block[0].reshape(groups, stride_rows, width),
        row_block[1].reshape(groups, stride_rows, width),
        labels.reshape(groups, stride_rows, tile_cols),
    )
    running, left_terms = lax.scan(advance, start, records)
    grad_left = lax.psum_scatter(
        left_terms.reshape(tile_rows, width), "col", scatter_dimension=0, tiled=True
    )
    grad_right = over_copies(running[3], "row")
    grad_in, grad_out, grad_bins = lax.psum((running[0], running[1], running[2]), ("row", "col"))
    residues = tile_rows * lax.axis_size("row")
    return (grad_left, grad_right, grad_in / residues, grad_out / residues, grad_bins / residues)


def solution(mesh):
    placed = (
        P(("row", "col"), None),
        P(("row", "col"), None),
        P(),
        P(),
        P(),
        P(),
        P(),
        P(),
        P("row", "col"),
    )
    return jax.shard_map(
        on_device,
        mesh=mesh,
        in_specs=placed,
        out_specs=(P(("row", "col"), None), P("col", None), P(), P(), P()),
        check_vma=False,
    )
```

profile of v0, /device:TPU:2, one launch (start us, length us, event | category | flops | bytes accessed | tf_op | source)
XLA Modules:
  0.0 512.4 jit_solution(3659964022238284578)
XLA Ops:
  7.2 0.7 pad_maximum_fusion
  8.5 6.2 %all-to-all-start = ((bf16[16,2,6,128]{3,1,2,0:T(2,128)(2,1)}), bf16[16,2,6,128]{3,1,2,0:T(2,128)(2,1)S(1)}, u32[]{:S(2)}, u32[]{:S(2)}) async-start(bf16[16,2,6,128]{3,1,2,0:T(2,128)(2,1)} %broadcast_in_dim.22), calls=%async_computation | async-start | bytes 98304 | tf_op jit(solution)/shard_map/all_to_all | solution.py:9
  14.8 4.7 all-to-all-done
  19.8 52.6 %all_gather.3 = bf16[16,2,96,128]{3,2,1,0:T(8,128)(2,1)S(1)} all-gather(bf16[1,2,96,128]{3,2,1,0:T(8,128)(2,1)S(1)} %copy.34), channel_id=1, replica_groups=mesh['row'=16,'col'=16] {'row'}, dimensions={0}, use_global_device_ids=true | all-gather | bytes 835584 | tf_op jit(solution)/shard_map/all_gather | solution.py:26
  72.4 161.3 %while.19 = (s32[]{:T(128)}, f32[128,512]{1,0:T(8,128)S(1)}, f32[512,128]{1,0:T(8,128)S(1)}, f32[128,64]{0,1:T(8,128)S(1)}, f32[96,128]{1,0:T(8,128)S(1)}, /*ind...) while((s32[]{:T(128)}, f32[128,512]{1,0:T(8,128)S(1)}, ...), condition=%wide.region_11.12_spmd.clone, body=%wide.region_0.11_spmd.clone.sunk | while | flops 869032064 | bytes 20266860 | solution.py:131
  74.2 1.9 fusion.121
  76.9 1.6 multiply_convert_fusion.5
  79.5 1.5 fusion.122
  81.8 2.1 multiply_convert_fusion.6
  85.8 0.7 constant_dynamic-slice_fusion.3
  87.7 1.9 fusion.121
  90.4 1.6 multiply_convert_fusion.5
  92.9 1.5 fusion.122
  95.2 2.1 multiply_convert_fusion.6
  99.3 0.7 constant_dynamic-slice_fusion.3
  101.1 1.9 fusion.121
  103.8 1.6 multiply_convert_fusion.5
  106.4 1.5 fusion.122
  108.6 2.1 multiply_convert_fusion.6
  114.5 1.9 fusion.121
  117.2 1.6 multiply_convert_fusion.5
  119.8 1.5 fusion.122
  122.1 2.1 multiply_convert_fusion.6
  128.0 1.9 fusion.121
  130.7 1.6 multiply_convert_fusion.5
  133.3 1.5 fusion.122
  135.5 2.1 multiply_convert_fusion.6
  141.4 1.9 fusion.121
  144.1 1.6 multiply_convert_fusion.5
  146.7 1.5 fusion.122
  149.0 2.1 multiply_convert_fusion.6
  154.9 1.9 fusion.121
  157.6 1.6 multiply_convert_fusion.5
  160.2 1.5 fusion.122
  162.4 2.1 multiply_convert_fusion.6
  168.3 1.9 fusion.121
  171.0 1.6 multiply_convert_fusion.5
  173.6 1.5 fusion.122
  175.9 2.1 multiply_convert_fusion.6
  179.9 0.7 constant_dynamic-slice_fusion.3
  181.8 1.9 fusion.121
  184.5 1.6 multiply_convert_fusion.5
  187.1 1.5 fusion.122
  189.3 2.1 multiply_convert_fusion.6
  195.2 1.9 fusion.121
  197.9 1.6 multiply_convert_fusion.5
  200.5 1.5 fusion.122
  202.7 2.1 multiply_convert_fusion.6
  206.8 0.7 constant_dynamic-slice_fusion.3
  208.7 1.9 fusion.121
  211.4 1.6 multiply_convert_fusion.5
  213.9 1.5 fusion.122
  216.2 2.1 multiply_convert_fusion.6
  222.1 1.9 fusion.121
  224.8 1.6 multiply_convert_fusion.5
  227.4 1.5 fusion.122
  229.6 2.1 multiply_convert_fusion.6
  233.7 1.0 broadcast_in_dim.23
  234.7 3.6 all-to-all-start.1
  239.7 55.0 %all-reduce = f32[96,128]{1,0:T(8,128)S(1)} all-reduce(f32[96,128]{1,0:T(8,128)S(1)} %bitcast.153), channel_id=2, replica_groups=mesh['row'=16,'col'=16] {'col'}, use_global_device_ids=true, to_apply=%region_12.13.clone | all-reduce | flops 12288 | bytes 98304
  295.3 79.4 %psum.23 = f32[128,64]{0,1:T(8,128)S(1)} all-reduce(f32[128,64]{0,1:T(8,128)S(1)} %get-tuple-element.95), channel_id=1, replica_groups=mesh['row'=16,'col'=16] {'row','col'}, use_global_device_ids=true, to_apply=%region_16.17 | all-reduce | flops 8192 | bytes 65536 | tf_op jit(solution)/shard_map/psum | solution.py:136
  375.3 126.2 %all-reduce.4.cloned.1.call-done = (f32[128,512]{1,0:T(8,128)}, f32[512,128]{1,0:T(8,128)}) async-done(((f32[128,512]{1,0:T(8,128)}, f32[512,128]{1,0:T(8,128)}), (f32[128,512]{1,0:T(8,128)}, f32[512,128]{1,0:T(8,128)})) %all-reduce.4.cloned.1.call-update) | async-done | bytes 524304 | tf_op jit(solution)/shard_map/psum | solution.py:136
  501.5 1.7 broadcast_multiply_fusion.5
  503.2 1.7 broadcast_multiply_fusion.4
  (573 shorter events, 73.1 us)
Async XLA Ops:
  8.5 10.9 %all-to-all-start = ((bf16[16,2,6,128]{3,1,2,0:T(2,128)(2,1)}), bf16[16,2,6,128]{3,1,2,0:T(2,128)(2,1)S(1)}, u32[]{:S(2)}, u32[]{:S(2)}) async-start(bf16[16,2,6,128]{3,1,2,0:T(2,128)(2,1)} %broadcast_in_dim.22), calls=%async_computation | async-start | bytes 98304 | tf_op jit(solution)/shard_map/all_to_all | solution.py:9
  74.2 2.4 copy-start.5
  74.2 2.4 copy-start.6
  74.2 2.7 copy-start.2
  74.2 2.7 copy-start.7
  76.9 2.0 copy-start.4
  87.6 2.4 copy-start.5
  87.6 2.4 copy-start.6
  87.6 2.7 copy-start.2
  87.6 2.7 copy-start.7
  90.3 2.0 copy-start.4
  101.0 2.4 copy-start.5
  101.1 2.4 copy-start.6
  101.1 2.7 copy-start.2
  101.1 2.7 copy-start.7
  103.8 2.0 copy-start.4
  114.5 2.4 copy-start.5
  114.5 2.4 copy-start.6
  114.5 2.7 copy-start.2
  114.5 2.7 copy-start.7
  117.2 2.0 copy-start.4
  127.9 2.4 copy-start.5
  128.0 2.4 copy-start.6
  128.0 2.7 copy-start.2
  128.0 2.7 copy-start.7
  130.7 2.0 copy-start.4
  141.4 2.4 copy-start.5
  141.4 2.4 copy-start.6
  141.4 2.7 copy-start.2
  141.4 2.7 copy-start.7
  144.1 2.0 copy-start.4
  154.8 2.4 copy-start.5
  154.8 2.4 copy-start.6
  154.9 2.7 copy-start.2
  154.9 2.7 copy-start.7
  157.6 2.0 copy-start.4
  168.3 2.4 copy-start.5
  168.3 2.4 copy-start.6
  168.3 2.7 copy-start.2
  168.3 2.7 copy-start.7
  171.0 2.0 copy-start.4
  181.7 2.4 copy-start.5
  181.7 2.4 copy-start.6
  181.7 2.7 copy-start.2
  181.8 2.7 copy-start.7
  184.5 2.0 copy-start.4
  195.2 2.4 copy-start.5
  195.2 2.4 copy-start.6
  195.2 2.7 copy-start.2
  195.2 2.7 copy-start.7
  208.6 2.4 copy-start.5
  208.6 2.4 copy-start.6
  208.6 2.7 copy-start.2
  208.6 2.7 copy-start.7
  211.3 2.0 copy-start.4
  222.0 2.4 copy-start.5
  222.1 2.4 copy-start.6
  222.1 2.7 copy-start.2
  222.1 2.7 copy-start.7
  233.7 6.0 %copy-start = (f32[512,128]{1,0:T(8,128)}, f32[512,128]{1,0:T(8,128)S(1)}, u32[]{:S(2)}) copy-start(f32[512,128]{1,0:T(8,128)S(1)} %get-tuple-element.94) | copy-start | bytes 786436
  233.7 6.0 %copy-start.1 = (f32[128,512]{1,0:T(8,128)}, f32[128,512]{1,0:T(8,128)S(1)}, u32[]{:S(2)}) copy-start(f32[128,512]{1,0:T(8,128)S(1)} %get-tuple-element.93) | copy-start | bytes 786436
  233.7 4.7 copy-start.8
  234.7 270.1 %all-to-all-start.1 = ((f32[16,96,128]{2,1,0:T(8,128)}), f32[16,96,128]{2,1,0:T(8,128)S(1)}, u32[]{:S(2)}, u32[]{:S(2)}) async-start(f32[16,96,128]{2,1,0:T(8,128)} %broadcast_in_dim.23), calls=%async_computation.1 | async-start | bytes 1572864 | tf_op jit(solution)/shard_map/all_to_all | solution.py:9
  238.4 263.2 %all-reduce.4.cloned.1.call-start = ((), (), s32[]{:S(2)}) async-start(), calls=%async_computation.2 | async-start | bytes 1048576 | tf_op jit(solution)/shard_map/psum | solution.py:136
  (14 other events, 24.0 us)
Sparse Core Ops, SparseCore 0:
  245.4 256.1 all-reduce.3
where the time goes:
time: 514 us; the launch traced here: 512 us
  blocking collectives  187 us (36%)
  waiting for transfers between devices  131 us (25%)
  matrix products  113 us (22%)
  other arithmetic  28 us (5%)
  local copies, waits for them, and re-layouts  25.2 us (5%)
  between operations  14.8 us (3%)
  starting transfers between devices  9.86 us (2%)
    psum x1, waiting for transfers between devices, on_device(): lax.psum((running[0], running[1], running[2]), ('row', 'col'))  126 us
    psum x1, blocking collectives, on_device(): lax.psum((running[0], running[1], running[2]), ('row', 'col'))  79.4 us
    unnamed x1, blocking collectives  55 us
    all_gather x1, blocking collectives, picked(): lax.all_gather(value, axis)  52.6 us
    dot_general x36, matrix products, outer(): lax.dot_general(first, second, (((1,), (1,)), ((), ())), preferred_elemen...  34.7 us
    dot_general x24, matrix products, transition(): jnp.dot(hidden, w_out, preferred_element_type=jnp.float32)  27.4 us
    dot_general x12, matrix products, transition(): pre_act = jnp.dot(normed, w_in, preferred_element_type=jnp.float32) + b_in  19.6 us
    div x12, matrix products, pair_backward(): probs = expo / jnp.sum(expo, axis=-1, keepdims=True)  17.9 us
  transfers between devices with their start and end apart: 3, of which 2 were waited for; matrix products, arithmetic and copies ran while one was open for 1% of the time, Pallas kernels for 0%

commit v1 on v0

--- a/solution.py
+++ b/solution.py
@@ -2,6 +2,14 @@
 import jax.numpy as jnp
 from jax import lax
 from jax.sharding import PartitionSpec as P
+
+
+def run_kinds(local_x):
+    named_axis = "row"
+    peer_axis = "col"
+    for tick in (peer_axis, named_axis):
+        local_x = lax.psum(local_x, tick)
+    return local_x
 
 
 def from_everyone(value, axis):
@@ -133,7 +141,7 @@
         left_terms.reshape(tile_rows, width), "col", scatter_dimension=0, tiled=True
     )
     grad_right = over_copies(running[3], "row")
-    grad_in, grad_out, grad_bins = lax.psum((running[0], running[1], running[2]), ("row", "col"))
+    grad_in, grad_out, grad_bins = run_kinds((running[0], running[1], running[2]))
     residues = tile_rows * lax.axis_size("row")
     return (grad_left, grad_right, grad_in / residues, grad_out / residues, grad_bins / residues)
 

time: 514 us -> 661 us (1.29)
  waiting for transfers between devices: 131 us -> 322 us
  blocking collectives: 187 us -> 136 us
  local copies, waits for them, and re-layouts: 25.2 us -> 33.6 us
    unnamed x1 -> x4, waiting for transfers between devices: 0.02 us -> 122 us
    psum x1 -> x2, waiting for transfers between devices: 126 us -> 195 us  [run_kinds(): local_x = lax.psum(local_x, tick)]
    unnamed x1 -> x0, blocking collectives: 55 us -> none
    dynamic_update_slice x12, local copies, waits for them, and re-layouts: 0.09 us -> 7.19 us  [on_device(): running, left_terms = lax.scan(advance, start, records)]
  transfers between devices with their start and end apart: 3 -> 5, of which waited for: 2 -> 4; matrix products, arithmetic and copies ran while one was open for 1% -> 1% of each run, Pallas kernels for 0% -> 0%
where the time goes in v1:
time: 661 us; the launch traced here: 659 us
  waiting for transfers between devices  322 us (49%)
  blocking collectives  136 us (21%)
  matrix products  113 us (17%)
  local copies, waits for them, and re-layouts  33.6 us (5%)
  other arithmetic  28 us (4%)
  between operations  14.5 us (2%)
  starting transfers between devices  9.93 us (2%)
    psum x2, waiting for transfers between devices, run_kinds(): local_x = lax.psum(local_x, tick)  195 us
    unnamed x4, waiting for transfers between devices  122 us
    psum x1, blocking collectives, run_kinds(): local_x = lax.psum(local_x, tick)  82.9 us
    all_gather x1, blocking collectives, picked(): lax.all_gather(value, axis)  52.6 us
    dot_general x36, matrix products, outer(): lax.dot_general(first, second, (((1,), (1,)), ((), ())), preferred_elemen...  34.6 us
    dot_general x24, matrix products, transition(): jnp.dot(hidden, w_out, preferred_element_type=jnp.float32)  27.3 us
    dot_general x12, matrix products, transition(): pre_act = jnp.dot(normed, w_in, preferred_element_type=jnp.float32) + b_in  19.6 us
    div x12, matrix products, pair_backward(): probs = expo / jnp.sum(expo, axis=-1, keepdims=True)  18 us
  transfers between devices with their start and end apart: 5, of which 4 were waited for; matrix products, arithmetic and copies ran while one was open for 1% of the time, Pallas kernels for 0%

profile of v1, /device:TPU:2, one launch (start us, length us, event | category | flops | bytes accessed | tf_op | source)
XLA Modules:
  0.0 659.4 jit_solution(14587531637248019851)
XLA Ops:
  7.2 0.7 pad_maximum_fusion
  8.5 6.2 all-to-all-start
  14.8 4.7 all-to-all-done
  19.8 52.6 %all_gather.3 = bf16[16,2,96,128]{3,2,1,0:T(8,128)(2,1)S(1)} all-gather(bf16[1,2,96,128]{3,2,1,0:T(8,128)(2,1)S(1)} %copy.34), channel_id=1, replica_groups=mesh['row'=16,'col'=16] {'row'}, dimensions={0}, use_global_device_ids=true | all-gather | bytes 835584 | tf_op jit(solution)/shard_map/all_gather | solution.py:34
  72.4 167.8 %while.19 = (s32[]{:T(128)}, f32[128,512]{1,0:T(8,128)S(1)}, f32[512,128]{1,0:T(8,128)S(1)}, f32[128,64]{0,1:T(8,128)S(1)}, f32[96,128]{1,0:T(8,128)S(1)}, /*ind...) while((s32[]{:T(128)}, f32[128,512]{1,0:T(8,128)S(1)}, ...), condition=%wide.region_11.12_spmd.clone, body=%wide.region_0.11_spmd.clone.sunk | while | flops 869032064 | bytes 20266860 | solution.py:139
  72.4 0.7 constant_dynamic-slice_fusion.3
  74.2 1.9 fusion.121
  76.9 1.6 multiply_convert_fusion.5
  79.5 1.5 fusion.122
  81.7 2.1 multiply_convert_fusion.6
  88.2 1.9 fusion.121
  90.9 1.6 multiply_convert_fusion.5
  93.5 1.5 fusion.122
  95.7 2.1 multiply_convert_fusion.6
  102.2 1.9 fusion.121
  104.9 1.6 multiply_convert_fusion.5
  107.5 1.5 fusion.122
  109.7 2.1 multiply_convert_fusion.6
  116.2 1.9 fusion.121
  118.9 1.6 multiply_convert_fusion.5
  121.4 1.5 fusion.122
  123.7 2.1 multiply_convert_fusion.6
  130.2 1.9 fusion.121
  132.9 1.6 multiply_convert_fusion.5
  135.4 1.5 fusion.122
  137.7 2.1 multiply_convert_fusion.6
  144.1 1.9 fusion.121
  146.8 1.6 multiply_convert_fusion.5
  149.4 1.5 fusion.122
  151.7 2.1 multiply_convert_fusion.6
  158.1 1.9 fusion.121
  160.8 1.6 multiply_convert_fusion.5
  163.4 1.5 fusion.122
  165.7 2.1 multiply_convert_fusion.6
  172.1 1.9 fusion.121
  174.8 1.6 multiply_convert_fusion.5
  177.4 1.5 fusion.122
  179.7 2.1 multiply_convert_fusion.6
  186.1 1.9 fusion.121
  188.8 1.6 multiply_convert_fusion.5
  191.4 1.5 fusion.122
  193.6 2.1 multiply_convert_fusion.6
  200.1 1.9 fusion.121
  202.8 1.6 multiply_convert_fusion.5
  205.4 1.5 fusion.122
  207.6 2.1 multiply_convert_fusion.6
  214.1 1.9 fusion.121
  216.8 1.6 multiply_convert_fusion.5
  219.4 1.5 fusion.122
  221.6 2.1 multiply_convert_fusion.6
  228.1 1.9 fusion.121
  230.8 1.6 multiply_convert_fusion.5
  233.3 1.5 fusion.122
  235.6 2.1 multiply_convert_fusion.6
  240.2 0.7 copy-done
  241.0 1.0 broadcast_in_dim.23
  242.0 3.6 all-to-all-start.1
  246.4 108.0 %all-reduce.10.cloned.1.call-done = (f32[128,512]{1,0:T(8,128)}, f32[512,128]{1,0:T(8,128)}) async-done(((f32[128,512]{1,0:T(8,128)}, f32[512,128]{1,0:T(8,128)}), (f32[128,512]{1,0:T(8,128)}, f32[512,128]{1,0:T(8,128)})) %all-reduce.10.cloned.1.call-update) | async-done | bytes 524304 | tf_op jit(solution)/shard_map/psum | solution.py:11
  355.7 121.6 %all-reduce.8.cloned.1.call-done = (f32[96,128]{1,0:T(8,128)}, f32[128,64]{0,1:T(8,128)}) async-done(((f32[96,128]{1,0:T(8,128)}, f32[128,64]{0,1:T(8,128)}), (f32[96,128]{1,0:T(8,128)}, f32[128,64]{0,1:T(8,128)})) %all-reduce.8.cloned.1.call-update) | async-done | bytes 81936
  477.3 82.9 %psum.47 = f32[128,64]{0,1:T(8,128)S(1)} all-reduce(f32[128,64]{0,1:T(8,128)} %get-tuple-element.234), channel_id=1, replica_groups=mesh['row'=16,'col'=16] {'row'}, use_global_device_ids=true, to_apply=%region_19.20 | all-reduce | flops 8192 | bytes 65536 | tf_op jit(solution)/shard_map/psum | solution.py:11
  560.3 1.3 constant_dynamic-slice_fusion.1
  562.2 86.6 %all-reduce.12.cloned.1.call-done = (f32[128,512]{1,0:T(8,128)}, f32[512,128]{1,0:T(8,128)}) async-done(((f32[128,512]{1,0:T(8,128)}, f32[512,128]{1,0:T(8,128)}), (f32[128,512]{1,0:T(8,128)}, f32[512,128]{1,0:T(8,128)})) %all-reduce.12.cloned.1.call-update) | async-done | bytes 524304 | tf_op jit(solution)/shard_map/psum | solution.py:11
  648.8 1.7 broadcast_multiply_fusion.5
  650.5 1.7 broadcast_multiply_fusion.4
  (580 shorter events, 82.4 us)
Async XLA Ops:
  8.5 10.9 %all-to-all-start = ((bf16[16,2,6,128]{3,1,2,0:T(2,128)(2,1)}), bf16[16,2,6,128]{3,1,2,0:T(2,128)(2,1)S(1)}, u32[]{:S(2)}, u32[]{:S(2)}) async-start(bf16[16,2,6,128]{3,1,2,0:T(2,128)(2,1)} %broadcast_in_dim.22), calls=%async_computation | async-start | bytes 98304 | tf_op jit(solution)/shard_map/all_to_all | solution.py:17
  14.7 339.7 %all-reduce.10.cloned.1.call-start = ((), (), s32[]{:S(2)}) async-start(), calls=%async_computation.3 | async-start | bytes 1048576 | tf_op jit(solution)/shard_map/psum | solution.py:11
  74.2 2.4 copy-start.6
  74.2 2.4 copy-start.7
  74.2 2.7 copy-start.2
  74.2 2.7 copy-start.8
  76.9 2.0 copy-start.4
  88.1 2.4 copy-start.6
  88.2 2.4 copy-start.7
  88.2 2.7 copy-start.2
  88.2 2.7 copy-start.8
  102.1 2.4 copy-start.6
  102.1 2.4 copy-start.7
  102.2 2.7 copy-start.2
  102.2 2.7 copy-start.8
  104.9 2.0 copy-start.4
  116.1 2.4 copy-start.6
  116.1 2.4 copy-start.7
  116.1 2.7 copy-start.2
  116.2 2.7 copy-start.8
  118.9 2.0 copy-start.4
  130.1 2.4 copy-start.6
  130.1 2.4 copy-start.7
  130.1 2.7 copy-start.2
  130.1 2.7 copy-start.8
  132.8 2.0 copy-start.4
  144.1 2.4 copy-start.6
  144.1 2.4 copy-start.7
  144.1 2.7 copy-start.2
  144.1 2.7 copy-start.8
  146.8 2.0 copy-start.4
  158.1 2.4 copy-start.6
  158.1 2.4 copy-start.7
  158.1 2.7 copy-start.2
  158.1 2.7 copy-start.8
  160.8 2.0 copy-start.4
  172.1 2.4 copy-start.6
  172.1 2.4 copy-start.7
  172.1 2.7 copy-start.2
  172.1 2.7 copy-start.8
  174.8 2.0 copy-start.4
  186.1 2.4 copy-start.6
  186.1 2.4 copy-start.7
  186.1 2.7 copy-start.2
  186.1 2.7 copy-start.8
  188.8 2.0 copy-start.4
  200.0 2.4 copy-start.6
  200.1 2.4 copy-start.7
  200.1 2.7 copy-start.2
  200.1 2.7 copy-start.8
  202.8 2.0 copy-start.4
  214.0 2.4 copy-start.6
  214.0 2.4 copy-start.7
  214.1 2.7 copy-start.2
  214.1 2.7 copy-start.8
  228.0 2.4 copy-start.6
  228.0 2.4 copy-start.7
  228.0 2.7 copy-start.2
  228.1 2.7 copy-start.8
  240.2 5.4 copy-start.5
  241.0 113.5 %copy-start.9 = (u32[256]{0:T(256)S(1)}, u32[256]{0:T(256)}, u32[]{:S(2)}) copy-start(u32[256]{0:T(256)} %constant.59) | copy-start | bytes 3076
  242.0 410.2 %all-to-all-start.1 = ((f32[16,96,128]{2,1,0:T(8,128)}), f32[16,96,128]{2,1,0:T(8,128)S(1)}, u32[]{:S(2)}, u32[]{:S(2)}) async-start(f32[16,96,128]{2,1,0:T(8,128)} %broadcast_in_dim.23), calls=%async_computation.1 | async-start | bytes 1572864 | tf_op jit(solution)/shard_map/all_to_all | solution.py:17
  245.6 231.7 %all-reduce.8.cloned.1.call-start = ((), (), s32[]{:S(2)}) async-start(), calls=%async_computation.2 | async-start | bytes 163840
  246.4 402.4 %all-reduce.12.cloned.1.call-start = ((), (), s32[]{:S(2)}) async-start(), calls=%async_computation.4 | async-start | bytes 1048576 | tf_op jit(solution)/shard_map/psum | solution.py:11
  (17 other events, 27.5 us)
Sparse Core Ops, SparseCore 0:
  241.1 113.2 all-reduce.9
  357.7 119.5 all-reduce.7
  480.0 168.7 all-reduce.11
